TPU v7x, 32 devices: a whole 2x2x4 slice. The times are simulated.
32 devices in a mesh: gx: 4 (over y, x), gy: 8 (over z, core).
Axes of the slice: x: 2, y: 2, z: 4, core: 2. Of those that a mesh axis runs over, the one named last changes fastest.
Arguments:
- features: bfloat16 [32, 32, 64, 128], P(None, 'gx', 'gy'), may hold values from -6 to 6
- weight_two: bfloat16 [27, 32, 32], replicated, may hold values from -0.21875 to 0.21875
- bias_two: float32 [32], replicated, may hold values from -3 to 3
- weight_three: bfloat16 [27, 64, 32], replicated, may hold values from -0.21875 to 0.21875
- bias_three: float32 [64], replicated, may hold values from -3 to 3
- weight_four: bfloat16 [27, 128, 64], replicated, may hold values from -0.25 to 0.25
- bias_four: float32 [128], replicated, may hold values from -3 to 3
Outputs:
- level_two: bfloat16 [32, 32, 64, 128], P(None, 'gx', 'gy')
- level_three: bfloat16 [64, 16, 32, 64], P(None, 'gx', 'gy')
- bottleneck: bfloat16 [128, 8, 16, 32], P(None, None, None, 'gy')
All inputs are finite; a program needn't handle non-finite values.
Results may differ from a plain program's by a relative error of at most 0.0085.
Values may be sent and summed in bfloat16 or wider, within the bound.
No kernel may reach another device: no remote copies, remote signals or barrier semaphores. Data moves between devices by JAX's collectives and lax.ppermute only.
A program may use at most 64 MiB of HBM per device.

v0:
```python
import jax
import jax.numpy as jnp
from jax import lax
from jax.sharding import PartitionSpec as P


def extended(cells, sides, width):
    for axis, dim in sides:
        count = lax.axis_size(axis)
        head = lax.slice_in_dim(cells, 0, width, axis=dim)
        tail = lax.slice_in_dim(cells, cells.shape[dim] - width, cells.shape[dim], axis=dim)
        cells = jnp.concatenate(
            [
                lax.ppermute(tail, axis, [(i, (i + 1) % count) for i in range(count)]),
                cells,
                lax.ppermute(head, axis, [((i + 1) % count, i) for i in range(count)]),
            ],
            axis=dim,
        )
    return cells


def wrap_axis(source, axis):
    first = lax.slice_in_dim(source, 0, 1, axis=axis)
    final = lax.slice_in_dim(source, source.shape[axis] - 1, source.shape[axis], axis=axis)
    return jnp.concatenate([final, source, first], axis=axis)


def convolve(padded, weights, bias_values):
    in_channels = padded.shape[0]
    extent_x = padded.shape[1] - 2
    extent_y = padded.shape[2] - 2
    extent_z = padded.shape[3] - 2
    out_channels = weights.shape[1]
    running = jnp.zeros((out_channels, extent_x * extent_y * extent_z), jnp.float32)
    for offset_x in range(3):
        for offset_y in range(3):
            stacked = jnp.concatenate(
                [
                    padded[
                        :,
                        offset_x : offset_x + extent_x,
                        offset_y : offset_y + extent_y,
                        offset_z : offset_z + extent_z,
                    ]
                    for offset_z in range(3)
                ],
                axis=0,
            ).reshape(3 * in_channels, -1)
            first_row = offset_x * 9 + offset_y * 3
            mixing = (
                weights[first_row : first_row + 3]
                .transpose(1, 0, 2)
                .reshape(out_channels, 3 * in_channels)
            )
            running = running + jnp.dot(mixing, stacked, preferred_element_type=jnp.float32)
    result = running + bias_values[:, None]
    result = jax.nn.leaky_relu(result, 0.1).astype(jnp.bfloat16)
    return result.reshape(out_channels, extent_x, extent_y, extent_z)


def average_pool(source):
    channels, extent_x, extent_y, extent_z = source.shape
    blocks = source.astype(jnp.float32).reshape(
        channels, extent_x // 2, 2, extent_y // 2, 2, extent_z // 2, 2
    )
    return blocks.mean(axis=(2, 4, 6)).astype(jnp.bfloat16)


def shards(features, weight_two, bias_two, weight_three, bias_three, weight_four, bias_four):
    rimmed = extended(features, (("gx", 1), ("gy", 2)), 1)
    level_two = convolve(wrap_axis(rimmed, 3), weight_two, bias_two)
    pooled = average_pool(level_two)
    rimmed_three = extended(pooled, (("gx", 1), ("gy", 2)), 1)
    level_three = convolve(wrap_axis(rimmed_three, 3), weight_three, bias_three)
    coarse = average_pool(level_three)
    pieces = lax.all_to_all(coarse, "gy", split_axis=3, concat_axis=2, tiled=True)
    slab_rows = lax.all_gather(pieces, "gx", axis=1, tiled=True)
    deepened = extended(slab_rows, (("gy", 3),), 1)
    padded = wrap_axis(wrap_axis(deepened, 1), 2)
    bottleneck = convolve(padded, weight_four, bias_four)
    return (level_two, level_three, bottleneck)


def solution(mesh):
    return jax.shard_map(
        shards,
        mesh=mesh,
        in_specs=(P(None, "gx", "gy", None), P(), P(), P(), P(), P(), P()),
        out_specs=(P(None, "gx", "gy", None), P(None, "gx", "gy", None), P(None, None, None, "gy")),
        check_vma=False,
    )
```

profile of v0, /device:TPU:0, one launch (start us, length us, event | category | flops | bytes accessed | tf_op | source)
XLA Modules:
  0.0 100.0 jit_solution(3070848087950724654)
XLA Ops:
  0.6 1.5 %copy.174 = bf16[32,8,8,128]{3,0,2,1:T(8,128)(2,1)S(1)} copy(bf16[32,8,8,128]{3,2,1,0:T(8,128)(2,1)} %param.7) | data formatting | bytes 1048576 | tf_op args[0]
  2.1 3.0 %collective-permute-start = (bf16[32,1,8,128]{3,0,2,1:T(8,128)(2,1)S(1)}, bf16[32,1,8,128]{3,0,2,1:T(8,128)(2,1)S(1)}, u32[]{:S(2)}, u32[]{:S(2)}) collective-permute-start(bf16[32,1,8,128]{3,0,2,1:T(8,128)(2,1)S(1)} %get-tuple-element.57), channel_id=1, source_target_pairs={{0,8},{8,16},{16,24},{24,0},{1,9},{9,17},{17,25},{25,1},{2,10},{10... | collective-permute-start | bytes 196616 | tf_op jit(solution)/shard_map/ppermute | solution.py:14
  5.1 1.0 %collective-permute-start.1 = (bf16[32,1,8,128]{3,0,2,1:T(8,128)(2,1)S(1)}, bf16[32,1,8,128]{3,0,2,1:T(8,128)(2,1)S(1)}, u32[]{:S(2)}, u32[]{:S(2)}) collective-permute-start(bf16[32,1,8,128]{3,0,2,1:T(8,128)(2,1)S(1)} %get-tuple-element.56), channel_id=1, source_target_pairs={{8,0},{16,8},{24,16},{0,24},{9,1},{17,9},{25,17},{1,25},{10,2},{18... | collective-permute-start | bytes 196616 | tf_op jit(solution)/shard_map/ppermute | solution.py:16
  6.2 2.3 %collective-permute-done = bf16[32,1,8,128]{3,0,2,1:T(8,128)(2,1)S(1)} collective-permute-done((bf16[32,1,8,128]{3,0,2,1:T(8,128)(2,1)S(1)}, bf16[32,1,8,128]{3,0,2,1:T(8,128)(2,1)S(1)}, u32[]{:S(2)}, u32[]{:S(2)}) %collective-permute-start) | collective-permute-done | bytes 65568 | tf_op jit(solution)/shard_map/ppermute | solution.py:14
  8.8 1.0 %collective-permute-done.1 = bf16[32,1,8,128]{3,0,2,1:T(8,128)(2,1)S(1)} collective-permute-done((bf16[32,1,8,128]{3,0,2,1:T(8,128)(2,1)S(1)}, bf16[32,1,8,128]{3,0,2,1:T(8,128)(2,1)S(1)}, u32[]{:S(2)}, u32[]{:S(2)}) %collective-permute-start.1) | collective-permute-done | bytes 65568 | tf_op jit(solution)/shard_map/ppermute | solution.py:16
  9.9 2.2 %collective-permute-start.3 = (bf16[32,10,1,128]{3,0,2,1:T(8,128)(2,1)S(1)}, bf16[32,10,1,128]{3,0,2,1:T(8,128)(2,1)S(1)}, u32[]{:S(2)}, u32[]{:S(2)}) collective-permute-start(bf16[32,10,1,128]{3,0,2,1:T(8,128)(2,1)S(1)} %get-tuple-element.52), channel_id=1, source_target_pairs={{1,0},{2,1},{3,2},{4,3},{5,4},{6,5},{7,6},{0,7},{9,8},{10,9},{11,1... | collective-permute-start | bytes 245768 | tf_op jit(solution)/shard_map/ppermute | solution.py:16
  13.2 1.0 %collective-permute-done.3 = bf16[32,10,1,128]{3,0,2,1:T(8,128)(2,1)S(1)} collective-permute-done((bf16[32,10,1,128]{3,0,2,1:T(8,128)(2,1)S(1)}, bf16[32,10,1,128]{3,0,2,1:T(8,128)(2,1)S(1)}, u32[]{:S(2)}, u32[]{:S(2)}) %collective-permute-start.3) | collective-permute-done | bytes 81952 | tf_op jit(solution)/shard_map/ppermute | solution.py:16
  14.2 3.6 %collective-permute-done.2 = bf16[32,10,1,128]{3,0,2,1:T(8,128)(2,1)S(1)} collective-permute-done((bf16[32,10,1,128]{3,0,2,1:T(8,128)(2,1)S(1)}, bf16[32,10,1,128]{3,0,2,1:T(8,128)(2,1)S(1)}, u32[]{:S(2)}, u32[]{:S(2)}) %collective-permute-start.2) | collective-permute-done | bytes 81952 | tf_op jit(solution)/shard_map/ppermute | solution.py:14
  18.2 1.7 %maximum_maximum_fusion = (bf16[32,10,10,129]{3,0,2,1:T(8,128)(2,1)S(1)}, bf16[32,10,10,129]{3,0,2,1:T(8,128)(2,1)S(1)}) fusion(bf16[32,10,1,128]{3,0,2,1:T(8,128)(2,1)S(1)} %collective-permute-done.3, bf16[32,10,8,128]{3,0,2,1:T(8,128)(2,1)S(1)} %constant_dynamic-update-slice_fusion, bf16[32,10,1,128]{3,0,2,1:T(8,128)(2,1)S(1)} %collective-permute-done.2, ...), kind=kLoop, calls=%fused_computation.11 | loop fusion | flops 6604800 | bytes 2483200 | tf_op jit(solution)/shard_map/concatenate | solution.py:26
  19.9 2.8 %fusion.60 = (bf16[32,8,8,128]{3,0,2,1:T(8,128)(2,1)S(1)}, bf16[32,8,8,128]{3,0,2,1:T(8,128)(2,1)S(1)}, bf16[32,8,8,128]{3,0,2,1:T(8,128)(2,1)S(1)}, bf16[32,8,8...) fusion(bf16[32,10,10,129]{3,0,2,1:T(8,128)(2,1)S(1)} %get-tuple, ...), kind=kLoop, calls=%fused_computation.164 | loop fusion | bytes 18874368 | tf_op jit(solution)/shard_map/slice | solution.py:40
  30.0 1.1 %fusion.18 = f32[8192,32]{0,1:T(8,128)S(1)} fusion(bf16[32,96]{1,0:T(8,128)(2,1)S(1)} %reshape.189, bf16[12,8,64,128]{3,2,1,0:T(8,128)(2,1)S(1)} %bitcast.226), kind=kOutput, calls=%fused_computation.29 | convolution fusion | flops 50331648 | bytes 2627584 | tf_op jit(solution)/shard_map/dot_general | solution.py:56
  31.1 1.1 %convolution_add_fusion.7 = f32[8192,32]{0,1:T(8,128)S(1)} fusion(f32[8192,32]{0,1:T(8,128)S(1)} %fusion.18, bf16[32,96]{1,0:T(8,128)(2,1)S(1)} %reshape.191, bf16[12,8,64,128]{3,2,1,0:T(8,128)(2,1)S(1)} %bitcast.227), kind=kOutput, calls=%fused_computation.9 | convolution fusion | flops 50593792 | bytes 3676160 | tf_op jit(solution)/shard_map/dot_general | solution.py:56
  32.2 1.1 %convolution_add_fusion.6 = f32[8192,32]{0,1:T(8,128)S(1)} fusion(f32[8192,32]{0,1:T(8,128)S(1)} %convolution_add_fusion.7, bf16[32,96]{1,0:T(8,128)(2,1)S(1)} %reshape.193, bf16[12,8,64,128]{3,2,1,0:T(8,128)(2,1)S(1)} %bitcast.228), kind=kOutput, calls=%fused_computation.8 | convolution fusion | flops 50593792 | bytes 3676160 | tf_op jit(solution)/shard_map/dot_general | solution.py:56
  33.4 1.1 %convolution_add_fusion.5 = f32[8192,32]{0,1:T(8,128)S(1)} fusion(f32[8192,32]{0,1:T(8,128)S(1)} %convolution_add_fusion.6, bf16[32,96]{1,0:T(8,128)(2,1)S(1)} %reshape.195, bf16[12,8,64,128]{3,2,1,0:T(8,128)(2,1)S(1)} %bitcast.230), kind=kOutput, calls=%fused_computation.7 | convolution fusion | flops 50593792 | bytes 3676160 | tf_op jit(solution)/shard_map/dot_general | solution.py:56
  34.5 1.1 %convolution_add_fusion.4 = f32[8192,32]{0,1:T(8,128)S(1)} fusion(f32[8192,32]{0,1:T(8,128)S(1)} %convolution_add_fusion.5, bf16[32,96]{1,0:T(8,128)(2,1)S(1)} %reshape.197, bf16[12,8,64,128]{3,2,1,0:T(8,128)(2,1)S(1)} %bitcast.229), kind=kOutput, calls=%fused_computation.6 | convolution fusion | flops 50593792 | bytes 3676160 | tf_op jit(solution)/shard_map/dot_general | solution.py:56
  35.6 1.1 %convolution_add_fusion.3 = f32[8192,32]{0,1:T(8,128)S(1)} fusion(f32[8192,32]{0,1:T(8,128)S(1)} %convolution_add_fusion.4, bf16[32,96]{1,0:T(8,128)(2,1)S(1)} %reshape.199, bf16[12,8,64,128]{3,2,1,0:T(8,128)(2,1)S(1)} %bitcast.231), kind=kOutput, calls=%fused_computation.5 | convolution fusion | flops 50593792 | bytes 3676160 | tf_op jit(solution)/shard_map/dot_general | solution.py:56
  36.7 1.1 %convolution_add_fusion.2 = f32[8192,32]{0,1:T(8,128)S(1)} fusion(f32[8192,32]{0,1:T(8,128)S(1)} %convolution_add_fusion.3, bf16[32,96]{1,0:T(8,128)(2,1)S(1)} %reshape.201, bf16[12,8,64,128]{3,2,1,0:T(8,128)(2,1)S(1)} %bitcast.233), kind=kOutput, calls=%fused_computation.4 | convolution fusion | flops 50593792 | bytes 3676160 | tf_op jit(solution)/shard_map/dot_general | solution.py:56
  37.9 1.1 %convolution_add_fusion.1 = f32[8192,32]{0,1:T(8,128)S(1)} fusion(f32[8192,32]{0,1:T(8,128)S(1)} %convolution_add_fusion.2, bf16[32,96]{1,0:T(8,128)(2,1)S(1)} %reshape.203, bf16[12,8,64,128]{3,2,1,0:T(8,128)(2,1)S(1)} %bitcast.232), kind=kOutput, calls=%fused_computation.3 | convolution fusion | flops 50593792 | bytes 3676160 | tf_op jit(solution)/shard_map/dot_general | solution.py:56
  39.0 1.1 %fusion.31 = bf16[32,8192]{1,0:T(8,128)(2,1)S(1)} fusion(f32[8192,32]{0,1:T(8,128)S(1)} %convolution_add_fusion.1, bf16[32,96]{1,0:T(8,128)(2,1)S(1)} %reshape.205, bf16[12,8,64,128]{3,2,1,0:T(8,128)(2,1)S(1)} %bitcast.234, f32[32]{0:T(128)S(1)} %copy-done.13), kind=kOutput, calls=%fused_computation.49 | convolution fusion | flops 51904512 | bytes 3152000 | tf_op jit(solution)/shard_map/dot_general | solution.py:56
  40.1 2.4 %copy.198 = f32[32,8192]{0,1:T(8,128)} copy(bf16[32,8192]{1,0:T(8,128)(2,1)S(1)} %fusion.31) | data formatting | bytes 1572864 | tf_op jit(solution)/shard_map/convert_element_type | solution.py:64
  42.5 4.8 %reduce_sum.18 = f32[32,4,4,64]{0,3,2,1:T(8,128)S(1)} reduce(f32[32,4,2,4,2,64,2]{0,6,5,4,3,2,1:T(2,128)} %bitcast.225, f32[]{:T(128)} %constant.6.clone.1), dimensions={2,4,6}, to_apply=%region_0.1 | reduce | flops 229376 | bytes 1179652 | tf_op jit(solution)/shard_map/reduce_sum | solution.py:67
  47.4 2.1 %collective-permute-start.5 = (bf16[32,1,4,64]{0,3,2,1:T(8,128)(2,1)S(1)}, bf16[32,1,4,64]{0,3,2,1:T(8,128)(2,1)S(1)}, u32[]{:S(2)}, u32[]{:S(2)}) collective-permute-start(bf16[32,1,4,64]{0,3,2,1:T(8,128)(2,1)S(1)} %get-tuple-element.99), channel_id=1, source_target_pairs={{8,0},{16,8},{24,16},{0,24},{9,1},{17,9},{25,17},{1,25},{10,2},{18... | collective-permute-start | bytes 49160 | tf_op jit(solution)/shard_map/ppermute | solution.py:16
  49.6 2.2 %collective-permute-done.5 = bf16[32,1,4,64]{0,3,2,1:T(8,128)(2,1)S(1)} collective-permute-done((bf16[32,1,4,64]{0,3,2,1:T(8,128)(2,1)S(1)}, bf16[32,1,4,64]{0,3,2,1:T(8,128)(2,1)S(1)}, u32[]{:S(2)}, u32[]{:S(2)}) %collective-permute-start.5) | collective-permute-done | bytes 16416 | tf_op jit(solution)/shard_map/ppermute | solution.py:16
  51.8 2.9 %collective-permute-done.4 = bf16[32,1,4,64]{0,3,2,1:T(8,128)(2,1)S(1)} collective-permute-done((bf16[32,1,4,64]{0,3,2,1:T(8,128)(2,1)S(1)}, bf16[32,1,4,64]{0,3,2,1:T(8,128)(2,1)S(1)}, u32[]{:S(2)}, u32[]{:S(2)}) %collective-permute-start.4) | collective-permute-done | bytes 16416 | tf_op jit(solution)/shard_map/ppermute | solution.py:14
  55.3 2.5 %collective-permute-done.7 = bf16[32,6,1,64]{0,3,2,1:T(8,128)(2,1)S(1)} collective-permute-done((bf16[32,6,1,64]{0,3,2,1:T(8,128)(2,1)S(1)}, bf16[32,6,1,64]{0,3,2,1:T(8,128)(2,1)S(1)}, u32[]{:S(2)}, u32[]{:S(2)}) %collective-permute-start.7) | collective-permute-done | bytes 24608 | tf_op jit(solution)/shard_map/ppermute | solution.py:16
  57.8 2.9 %collective-permute-done.6 = bf16[32,6,1,64]{0,3,2,1:T(8,128)(2,1)S(1)} collective-permute-done((bf16[32,6,1,64]{0,3,2,1:T(8,128)(2,1)S(1)}, bf16[32,6,1,64]{0,3,2,1:T(8,128)(2,1)S(1)}, u32[]{:S(2)}, u32[]{:S(2)}) %collective-permute-start.6) | collective-permute-done | bytes 24608 | tf_op jit(solution)/shard_map/ppermute | solution.py:14
  67.9 8.0 %all_to_all.18 = bf16[8,2,512]{2,1,0:T(2,128)(2,1)S(1)} all-to-all(bf16[8,2,512]{2,1,0:T(2,128)(2,1)S(1)} %reshape.247), channel_id=1, replica_groups=mesh['gx'=4,'gy'=8] {'gy'}, dimensions={0} | all-to-all | bytes 32768 | tf_op jit(solution)/shard_map/all_to_all | solution.py:77
  76.0 8.5 %all_gather.3 = bf16[64,8,16,4]{0,2,3,1:T(8,128)(2,1)S(1)} all-gather(bf16[64,2,16,4]{0,2,3,1:T(8,128)(2,1)S(1)} %bitcast.257), channel_id=1, replica_groups=mesh['gx'=4,'gy'=8] {'gx'}, dimensions={1}, use_global_device_ids=true | all-gather | bytes 81920 | tf_op jit(solution)/shard_map/all_gather | solution.py:78
  85.3 0.9 copy.221
  86.2 0.9 reshape.225
  87.1 3.5 %collective-permute-start.9 = (bf16[64,8,16,1]{0,2,3,1:T(8,128)(2,1)S(1)}, bf16[64,8,16,1]{0,2,3,1:T(8,128)(2,1)S(1)}, u32[]{:S(2)}, u32[]{:S(2)}) collective-permute-start(bf16[64,8,16,1]{0,2,3,1:T(8,128)(2,1)S(1)} %get-tuple-element.130), channel_id=1, source_target_pairs={{1,0},{2,1},{3,2},{4,3},{5,4},{6,5},{7,6},{0,7},{9,8},{10,9},{11,1... | collective-permute-start | bytes 49160 | tf_op jit(solution)/shard_map/ppermute | solution.py:16
  90.7 1.6 %collective-permute-done.9 = bf16[64,8,16,1]{0,2,3,1:T(8,128)(2,1)S(1)} collective-permute-done((bf16[64,8,16,1]{0,2,3,1:T(8,128)(2,1)S(1)}, bf16[64,8,16,1]{0,2,3,1:T(8,128)(2,1)S(1)}, u32[]{:S(2)}, u32[]{:S(2)}) %collective-permute-start.9) | collective-permute-done | bytes 16416 | tf_op jit(solution)/shard_map/ppermute | solution.py:16
  (156 shorter events, 25.2 us)
Async XLA Ops:
  0.6 7.8 %copy-start = (bf16[32,8,8,128]{3,2,1,0:T(8,128)(2,1)S(1)}, bf16[32,8,8,128]{3,2,1,0:T(8,128)(2,1)}, u32[]{:S(2)}) copy-start(bf16[32,8,8,128]{3,2,1,0:T(8,128)(2,1)} %param.7) | copy-start | bytes 1572868
  0.6 11.5 %copy-start.2 = (bf16[27,32,32]{2,1,0:T(8,128)(2,1)S(1)}, bf16[27,32,32]{2,1,0:T(8,128)(2,1)}, u32[]{:S(2)}) copy-start(bf16[27,32,32]{2,1,0:T(8,128)(2,1)} %param.8) | copy-start | bytes 165892
  2.1 6.3 %collective-permute-start = (bf16[32,1,8,128]{3,0,2,1:T(8,128)(2,1)S(1)}, bf16[32,1,8,128]{3,0,2,1:T(8,128)(2,1)S(1)}, u32[]{:S(2)}, u32[]{:S(2)}) collective-permute-start(bf16[32,1,8,128]{3,0,2,1:T(8,128)(2,1)S(1)} %get-tuple-element.57), channel_id=1, source_target_pairs={{0,8},{8,16},{16,24},{24,0},{1,9},{9,17},{17,25},{25,1},{2,10},{10... | collective-permute-start | bytes 196616 | tf_op jit(solution)/shard_map/ppermute | solution.py:14
  5.1 4.7 %collective-permute-start.1 = (bf16[32,1,8,128]{3,0,2,1:T(8,128)(2,1)S(1)}, bf16[32,1,8,128]{3,0,2,1:T(8,128)(2,1)S(1)}, u32[]{:S(2)}, u32[]{:S(2)}) collective-permute-start(bf16[32,1,8,128]{3,0,2,1:T(8,128)(2,1)S(1)} %get-tuple-element.56), channel_id=1, source_target_pairs={{8,0},{16,8},{24,16},{0,24},{9,1},{17,9},{25,17},{1,25},{10,2},{18... | collective-permute-start | bytes 196616 | tf_op jit(solution)/shard_map/ppermute | solution.py:16
  9.9 4.3 %collective-permute-start.3 = (bf16[32,10,1,128]{3,0,2,1:T(8,128)(2,1)S(1)}, bf16[32,10,1,128]{3,0,2,1:T(8,128)(2,1)S(1)}, u32[]{:S(2)}, u32[]{:S(2)}) collective-permute-start(bf16[32,10,1,128]{3,0,2,1:T(8,128)(2,1)S(1)} %get-tuple-element.52), channel_id=1, source_target_pairs={{1,0},{2,1},{3,2},{4,3},{5,4},{6,5},{7,6},{0,7},{9,8},{10,9},{11,1... | collective-permute-start | bytes 245768 | tf_op jit(solution)/shard_map/ppermute | solution.py:16
  12.1 5.7 %collective-permute-start.2 = (bf16[32,10,1,128]{3,0,2,1:T(8,128)(2,1)S(1)}, bf16[32,10,1,128]{3,0,2,1:T(8,128)(2,1)S(1)}, u32[]{:S(2)}, u32[]{:S(2)}) collective-permute-start(bf16[32,10,1,128]{3,0,2,1:T(8,128)(2,1)S(1)} %get-tuple-element.51), channel_id=1, source_target_pairs={{0,1},{1,2},{2,3},{3,4},{4,5},{5,6},{6,7},{7,0},{8,9},{9,10},{10,1... | collective-permute-start | bytes 245768 | tf_op jit(solution)/shard_map/ppermute | solution.py:14
  37.8 1.1 %copy-start.13 = (f32[32]{0:T(128)S(1)}, f32[32]{0:T(128)}, u32[]{:S(2)}) copy-start(f32[32]{0:T(128)} %param.9) | copy-start | bytes 388
  47.3 7.9 %copy-start.3 = (bf16[27,64,32]{1,2,0:T(8,128)(2,1)S(1)}, bf16[27,64,32]{1,2,0:T(8,128)(2,1)}, u32[]{:S(2)}) copy-start(bf16[27,64,32]{1,2,0:T(8,128)(2,1)} %param.10) | copy-start | bytes 331780
  47.4 4.4 %collective-permute-start.5 = (bf16[32,1,4,64]{0,3,2,1:T(8,128)(2,1)S(1)}, bf16[32,1,4,64]{0,3,2,1:T(8,128)(2,1)S(1)}, u32[]{:S(2)}, u32[]{:S(2)}) collective-permute-start(bf16[32,1,4,64]{0,3,2,1:T(8,128)(2,1)S(1)} %get-tuple-element.99), channel_id=1, source_target_pairs={{8,0},{16,8},{24,16},{0,24},{9,1},{17,9},{25,17},{1,25},{10,2},{18... | collective-permute-start | bytes 49160 | tf_op jit(solution)/shard_map/ppermute | solution.py:16
  49.5 5.2 %collective-permute-start.4 = (bf16[32,1,4,64]{0,3,2,1:T(8,128)(2,1)S(1)}, bf16[32,1,4,64]{0,3,2,1:T(8,128)(2,1)S(1)}, u32[]{:S(2)}, u32[]{:S(2)}) collective-permute-start(bf16[32,1,4,64]{0,3,2,1:T(8,128)(2,1)S(1)} %get-tuple-element.98), channel_id=1, source_target_pairs={{0,8},{8,16},{16,24},{24,0},{1,9},{9,17},{17,25},{25,1},{2,10},{10... | collective-permute-start | bytes 49160 | tf_op jit(solution)/shard_map/ppermute | solution.py:14
  54.7 3.1 %collective-permute-start.7 = (bf16[32,6,1,64]{0,3,2,1:T(8,128)(2,1)S(1)}, bf16[32,6,1,64]{0,3,2,1:T(8,128)(2,1)S(1)}, u32[]{:S(2)}, u32[]{:S(2)}) collective-permute-start(bf16[32,6,1,64]{0,3,2,1:T(8,128)(2,1)S(1)} %get-tuple-element.76), channel_id=1, source_target_pairs={{1,0},{2,1},{3,2},{4,3},{5,4},{6,5},{7,6},{0,7},{9,8},{10,9},{11,1... | collective-permute-start | bytes 73736 | tf_op jit(solution)/shard_map/ppermute | solution.py:16
  54.8 5.9 %collective-permute-start.6 = (bf16[32,6,1,64]{0,3,2,1:T(8,128)(2,1)S(1)}, bf16[32,6,1,64]{0,3,2,1:T(8,128)(2,1)S(1)}, u32[]{:S(2)}, u32[]{:S(2)}) collective-permute-start(bf16[32,6,1,64]{0,3,2,1:T(8,128)(2,1)S(1)} %get-tuple-element.75), channel_id=1, source_target_pairs={{0,1},{1,2},{2,3},{3,4},{4,5},{5,6},{6,7},{7,0},{8,9},{9,10},{10,1... | collective-permute-start | bytes 73736 | tf_op jit(solution)/shard_map/ppermute | solution.py:14
  66.2 0.8 copy-start.11
  67.0 17.6 %copy-start.1 = (bf16[27,128,64]{1,2,0:T(8,128)(2,1)S(1)}, bf16[27,128,64]{1,2,0:T(8,128)(2,1)}, u32[]{:S(2)}) copy-start(bf16[27,128,64]{1,2,0:T(8,128)(2,1)} %param.12) | copy-start | bytes 1327108
  84.5 6.1 %collective-permute-start.8 = (bf16[64,8,16,1]{0,2,3,1:T(8,128)(2,1)S(1)}, bf16[64,8,16,1]{0,2,3,1:T(8,128)(2,1)S(1)}, u32[]{:S(2)}, u32[]{:S(2)}) collective-permute-start(bf16[64,8,16,1]{0,2,3,1:T(8,128)(2,1)S(1)} %get-tuple-element.131), channel_id=1, source_target_pairs={{0,1},{1,2},{2,3},{3,4},{4,5},{5,6},{6,7},{7,0},{8,9},{9,10},{10,1... | collective-permute-start | bytes 49160 | tf_op jit(solution)/shard_map/ppermute | solution.py:14
  87.1 5.1 %collective-permute-start.9 = (bf16[64,8,16,1]{0,2,3,1:T(8,128)(2,1)S(1)}, bf16[64,8,16,1]{0,2,3,1:T(8,128)(2,1)S(1)}, u32[]{:S(2)}, u32[]{:S(2)}) collective-permute-start(bf16[64,8,16,1]{0,2,3,1:T(8,128)(2,1)S(1)} %get-tuple-element.130), channel_id=1, source_target_pairs={{1,0},{2,1},{3,2},{4,3},{5,4},{6,5},{7,6},{0,7},{9,8},{10,9},{11,1... | collective-permute-start | bytes 49160 | tf_op jit(solution)/shard_map/ppermute | solution.py:16
  92.2 0.6 copy-start.9
  94.2 0.9 copy-start.10
  96.3 1.0 copy-start.8
  96.5 1.0 %copy-start.7 = (bf16[3,128,64]{1,2,0:T(8,128)(2,1)S(1)}, bf16[3,128,64]{1,2,0:T(8,128)(2,1)}, u32[]{:S(2)}) copy-start(bf16[3,128,64]{1,2,0:T(8,128)(2,1)} %get-tuple-element.70) | copy-start | bytes 147460
  96.8 0.9 copy-start.6
  97.0 1.0 %copy-start.5 = (bf16[3,128,64]{1,2,0:T(8,128)(2,1)S(1)}, bf16[3,128,64]{1,2,0:T(8,128)(2,1)}, u32[]{:S(2)}) copy-start(bf16[3,128,64]{1,2,0:T(8,128)(2,1)} %get-tuple-element.68) | copy-start | bytes 147460
  97.3 0.9 copy-start.4
  98.2 0.9 copy-start.12
where the time goes:
time: 100 us
  local copies, waits for them, and re-layouts  21.7 us (22%)
  waiting for transfers between devices  19.9 us (20%)
  blocking collectives  16.5 us (16%)
  matrix products  14.8 us (15%)
  other arithmetic  12.9 us (13%)
  starting transfers between devices  12.6 us (13%)
  between operations  1.59 us (2%)
    dot_general x27, matrix products, convolve(): jnp.dot(mixing, stacked, preferred_element_type=jnp.float32)  14.8 us
    ppermute x5, waiting for transfers between devices, extended(): lax.ppermute(tail, axis, [(i, (i + 1) % count) for i in range(count)])  11.6 us
    ppermute x5, starting transfers between devices, extended(): lax.ppermute(head, axis, [((i + 1) % count, i) for i in range(count)])  8.9 us
    all_gather x1, blocking collectives, shards(): slab_rows = lax.all_gather(pieces, 'gx', axis=1, tiled=True)  8.49 us
    ppermute x5, waiting for transfers between devices, extended(): lax.ppermute(head, axis, [((i + 1) % count, i) for i in range(count)])  8.26 us
    all_to_all x1, blocking collectives, shards(): lax.all_to_all(coarse, 'gy', split_axis=3, concat_axis=2, tiled=True)  8.02 us
    concatenate x18, local copies, waits for them, and re-layouts, convolve(): jnp.concatenate([padded[:, offset_x:offset_x + extent_x, offset_y:offset_...  6.73 us
    reduce_sum x2, other arithmetic, average_pool(): return blocks.mean(axis=(2, 4, 6)).astype(jnp.bfloat16)  5.15 us
  transfers between devices with their start and end apart: 10, of which 9 were waited for; matrix products, arithmetic and copies ran while one was open for 4% of the time, Pallas kernels for 0%

commit v1 on v0

--- a/solution.py
+++ b/solution.py
@@ -2,6 +2,17 @@
 import jax.numpy as jnp
 from jax import lax
 from jax.sharding import PartitionSpec as P
+
+
+def pass_along(shard, axis, dim):
+    count = lax.axis_size(axis)
+    route = [(i, (i + 1) % count) for i in range(count)]
+    parts = [shard]
+    for far in range(1, count):
+        parts = [lax.ppermute(parts[0], axis, route), *parts]
+    result = jnp.concatenate(parts, axis=dim)
+    shift = (lax.axis_index(axis) + 1) * parts[-1].shape[dim]
+    return jnp.roll(result, shift, axis=dim)
 
 
 def extended(cells, sides, width):
@@ -75,7 +86,7 @@
     level_three = convolve(wrap_axis(rimmed_three, 3), weight_three, bias_three)
     coarse = average_pool(level_three)
     pieces = lax.all_to_all(coarse, "gy", split_axis=3, concat_axis=2, tiled=True)
-    slab_rows = lax.all_gather(pieces, "gx", axis=1, tiled=True)
+    slab_rows = pass_along(pieces, "gx", 1)
     deepened = extended(slab_rows, (("gy", 3),), 1)
     padded = wrap_axis(wrap_axis(deepened, 1), 2)
     bottleneck = convolve(padded, weight_four, bias_four)

time: 100 us -> 104 us (1.040)
  waiting for transfers between devices: 19.9 us -> 35.7 us
  blocking collectives: 16.5 us -> 8.02 us
  starting transfers between devices: 12.6 us -> 9.78 us
    ppermute x0 -> x3, waiting for transfers between devices: none -> 12.4 us  [pass_along(): parts = [lax.ppermute(parts[0], axis, route), *parts]]
    all_gather x1 -> x0, blocking collectives: 8.49 us -> none  [shards(): slab_rows = lax.all_gather(pieces, 'gx', axis=1, tiled=True)]
    ppermute x5, waiting for transfers between devices: 11.6 us -> 15.5 us  [extended(): lax.ppermute(tail, axis, [(i, (i + 1) % count) for i in range(count)])]
    ppermute x5, starting transfers between devices: 8.9 us -> 5.43 us  [extended(): lax.ppermute(head, axis, [((i + 1) % count, i) for i in range(count)])]
    slice x7 -> x9, local copies, waits for them, and re-layouts: 4.85 us -> 5 us  [convolve(): padded[:, offset_x:offset_x + extent_x, offset_y:offset_y + extent_y, off...]
    unnamed x36 -> x27, local copies, waits for them, and re-layouts: 3.16 us -> 3.04 us
    concatenate x21 -> x22, other arithmetic: 5 us -> 5.07 us  [convolve(): jnp.concatenate([padded[:, offset_x:offset_x + extent_x, offset_y:offset_...]
    concatenate x5 -> x6, other arithmetic: 2.28 us -> 2.34 us  [wrap_axis(): return jnp.concatenate([final, source, first], axis=axis)]
  transfers between devices with their start and end apart: 10 -> 13, of which waited for: 9 -> 13; matrix products, arithmetic and copies ran while one was open for 4% -> 3% of each run, Pallas kernels for 0% -> 0%
where the time goes in v1:
time: 104 us
  waiting for transfers between devices  35.7 us (34%)
  local copies, waits for them, and re-layouts  21.1 us (20%)
  matrix products  14.8 us (14%)
  other arithmetic  13.1 us (13%)
  starting transfers between devices  9.78 us (9%)
  blocking collectives  8.02 us (8%)
  between operations  1.58 us (2%)
    ppermute x5, waiting for transfers between devices, extended(): lax.ppermute(tail, axis, [(i, (i + 1) % count) for i in range(count)])  15.5 us
    dot_general x27, matrix products, convolve(): jnp.dot(mixing, stacked, preferred_element_type=jnp.float32)  14.8 us
    ppermute x3, waiting for transfers between devices, pass_along(): parts = [lax.ppermute(parts[0], axis, route), *parts]  12.4 us
    all_to_all x1, blocking collectives, shards(): lax.all_to_all(coarse, 'gy', split_axis=3, concat_axis=2, tiled=True)  8.02 us
    ppermute x5, waiting for transfers between devices, extended(): lax.ppermute(head, axis, [((i + 1) % count, i) for i in range(count)])  7.78 us
    concatenate x18, local copies, waits for them, and re-layouts, convolve(): jnp.concatenate([padded[:, offset_x:offset_x + extent_x, offset_y:offset_...  6.73 us
    ppermute x5, starting transfers between devices, extended(): lax.ppermute(head, axis, [((i + 1) % count, i) for i in range(count)])  5.43 us
    reduce_sum x2, other arithmetic, average_pool(): return blocks.mean(axis=(2, 4, 6)).astype(jnp.bfloat16)  5.15 us
  transfers between devices with their start and end apart: 13, of which 13 were waited for; matrix products, arithmetic and copies ran while one was open for 3% of the time, Pallas kernels for 0%

profile of v1, /device:TPU:0, one launch (start us, length us, event | category | flops | bytes accessed | tf_op | source)
XLA Modules:
  0.0 104.1 jit_solution(6483933977915420068)
XLA Ops:
  0.6 1.5 %copy.174 = bf16[32,8,8,128]{3,0,2,1:T(8,128)(2,1)S(1)} copy(bf16[32,8,8,128]{3,2,1,0:T(8,128)(2,1)} %param.7) | data formatting | bytes 1048576 | tf_op args[0]
  2.1 3.0 %collective-permute-start = (bf16[32,1,8,128]{3,0,2,1:T(8,128)(2,1)S(1)}, bf16[32,1,8,128]{3,0,2,1:T(8,128)(2,1)S(1)}, u32[]{:S(2)}, u32[]{:S(2)}) collective-permute-start(bf16[32,1,8,128]{3,0,2,1:T(8,128)(2,1)S(1)} %get-tuple-element.57), channel_id=1, source_target_pairs={{0,8},{8,16},{16,24},{24,0},{1,9},{9,17},{17,25},{25,1},{2,10},{10... | collective-permute-start | bytes 196616 | tf_op jit(solution)/shard_map/ppermute | solution.py:25
  5.1 1.0 collective-permute-start.1
  6.2 2.3 %collective-permute-done = bf16[32,1,8,128]{3,0,2,1:T(8,128)(2,1)S(1)} collective-permute-done((bf16[32,1,8,128]{3,0,2,1:T(8,128)(2,1)S(1)}, bf16[32,1,8,128]{3,0,2,1:T(8,128)(2,1)S(1)}, u32[]{:S(2)}, u32[]{:S(2)}) %collective-permute-start) | collective-permute-done | bytes 65568 | tf_op jit(solution)/shard_map/ppermute | solution.py:25
  8.8 1.0 collective-permute-done.1
  9.9 2.2 %collective-permute-start.3 = (bf16[32,10,1,128]{3,0,2,1:T(8,128)(2,1)S(1)}, bf16[32,10,1,128]{3,0,2,1:T(8,128)(2,1)S(1)}, u32[]{:S(2)}, u32[]{:S(2)}) collective-permute-start(bf16[32,10,1,128]{3,0,2,1:T(8,128)(2,1)S(1)} %get-tuple-element.52), channel_id=1, source_target_pairs={{1,0},{2,1},{3,2},{4,3},{5,4},{6,5},{7,6},{0,7},{9,8},{10,9},{11,1... | collective-permute-start | bytes 245768 | tf_op jit(solution)/shard_map/ppermute | solution.py:27
  13.2 1.0 collective-permute-done.3
  14.2 3.6 %collective-permute-done.2 = bf16[32,10,1,128]{3,0,2,1:T(8,128)(2,1)S(1)} collective-permute-done((bf16[32,10,1,128]{3,0,2,1:T(8,128)(2,1)S(1)}, bf16[32,10,1,128]{3,0,2,1:T(8,128)(2,1)S(1)}, u32[]{:S(2)}, u32[]{:S(2)}) %collective-permute-start.2) | collective-permute-done | bytes 81952 | tf_op jit(solution)/shard_map/ppermute | solution.py:25
  18.2 1.7 %maximum_maximum_fusion = (bf16[32,10,10,129]{3,0,2,1:T(8,128)(2,1)S(1)}, bf16[32,10,10,129]{3,0,2,1:T(8,128)(2,1)S(1)}) fusion(bf16[32,10,1,128]{3,0,2,1:T(8,128)(2,1)S(1)} %collective-permute-done.3, bf16[32,10,8,128]{3,0,2,1:T(8,128)(2,1)S(1)} %constant_dynamic-update-slice_fusion, bf16[32,10,1,128]{3,0,2,1:T(8,128)(2,1)S(1)} %collective-permute-done.2, ...), kind=kLoop, calls=%fused_computation.11 | loop fusion | flops 6604800 | bytes 2483200 | tf_op jit(solution)/shard_map/concatenate | solution.py:37
  19.9 2.8 %fusion.54 = (bf16[32,8,8,128]{3,0,2,1:T(8,128)(2,1)S(1)}, bf16[32,8,8,128]{3,0,2,1:T(8,128)(2,1)S(1)}, bf16[32,8,8,128]{3,0,2,1:T(8,128)(2,1)S(1)}, bf16[32,8,8...) fusion(bf16[32,10,10,129]{3,0,2,1:T(8,128)(2,1)S(1)} %get-tuple, ...), kind=kLoop, calls=%fused_computation.167 | loop fusion | bytes 18874368 | tf_op jit(solution)/shard_map/slice | solution.py:51
  30.0 1.1 %fusion.18 = f32[8192,32]{0,1:T(8,128)S(1)} fusion(bf16[32,96]{1,0:T(8,128)(2,1)S(1)} %reshape.189, bf16[12,8,64,128]{3,2,1,0:T(8,128)(2,1)S(1)} %bitcast.226), kind=kOutput, calls=%fused_computation.29 | convolution fusion | flops 50331648 | bytes 2627584 | tf_op jit(solution)/shard_map/dot_general | solution.py:67
  31.1 1.1 %convolution_add_fusion.7 = f32[8192,32]{0,1:T(8,128)S(1)} fusion(f32[8192,32]{0,1:T(8,128)S(1)} %fusion.18, bf16[32,96]{1,0:T(8,128)(2,1)S(1)} %reshape.191, bf16[12,8,64,128]{3,2,1,0:T(8,128)(2,1)S(1)} %bitcast.227), kind=kOutput, calls=%fused_computation.9 | convolution fusion | flops 50593792 | bytes 3676160 | tf_op jit(solution)/shard_map/dot_general | solution.py:67
  32.2 1.1 %convolution_add_fusion.6 = f32[8192,32]{0,1:T(8,128)S(1)} fusion(f32[8192,32]{0,1:T(8,128)S(1)} %convolution_add_fusion.7, bf16[32,96]{1,0:T(8,128)(2,1)S(1)} %reshape.193, bf16[12,8,64,128]{3,2,1,0:T(8,128)(2,1)S(1)} %bitcast.228), kind=kOutput, calls=%fused_computation.8 | convolution fusion | flops 50593792 | bytes 3676160 | tf_op jit(solution)/shard_map/dot_general | solution.py:67
  33.4 1.1 %convolution_add_fusion.5 = f32[8192,32]{0,1:T(8,128)S(1)} fusion(f32[8192,32]{0,1:T(8,128)S(1)} %convolution_add_fusion.6, bf16[32,96]{1,0:T(8,128)(2,1)S(1)} %reshape.195, bf16[12,8,64,128]{3,2,1,0:T(8,128)(2,1)S(1)} %bitcast.230), kind=kOutput, calls=%fused_computation.7 | convolution fusion | flops 50593792 | bytes 3676160 | tf_op jit(solution)/shard_map/dot_general | solution.py:67
  34.5 1.1 %convolution_add_fusion.4 = f32[8192,32]{0,1:T(8,128)S(1)} fusion(f32[8192,32]{0,1:T(8,128)S(1)} %convolution_add_fusion.5, bf16[32,96]{1,0:T(8,128)(2,1)S(1)} %reshape.197, bf16[12,8,64,128]{3,2,1,0:T(8,128)(2,1)S(1)} %bitcast.229), kind=kOutput, calls=%fused_computation.6 | convolution fusion | flops 50593792 | bytes 3676160 | tf_op jit(solution)/shard_map/dot_general | solution.py:67
  35.6 1.1 %convolution_add_fusion.3 = f32[8192,32]{0,1:T(8,128)S(1)} fusion(f32[8192,32]{0,1:T(8,128)S(1)} %convolution_add_fusion.4, bf16[32,96]{1,0:T(8,128)(2,1)S(1)} %reshape.199, bf16[12,8,64,128]{3,2,1,0:T(8,128)(2,1)S(1)} %bitcast.231), kind=kOutput, calls=%fused_computation.5 | convolution fusion | flops 50593792 | bytes 3676160 | tf_op jit(solution)/shard_map/dot_general | solution.py:67
  36.7 1.1 %convolution_add_fusion.2 = f32[8192,32]{0,1:T(8,128)S(1)} fusion(f32[8192,32]{0,1:T(8,128)S(1)} %convolution_add_fusion.3, bf16[32,96]{1,0:T(8,128)(2,1)S(1)} %reshape.201, bf16[12,8,64,128]{3,2,1,0:T(8,128)(2,1)S(1)} %bitcast.233), kind=kOutput, calls=%fused_computation.4 | convolution fusion | flops 50593792 | bytes 3676160 | tf_op jit(solution)/shard_map/dot_general | solution.py:67
  37.9 1.1 %convolution_add_fusion.1 = f32[8192,32]{0,1:T(8,128)S(1)} fusion(f32[8192,32]{0,1:T(8,128)S(1)} %convolution_add_fusion.2, bf16[32,96]{1,0:T(8,128)(2,1)S(1)} %reshape.203, bf16[12,8,64,128]{3,2,1,0:T(8,128)(2,1)S(1)} %bitcast.232), kind=kOutput, calls=%fused_computation.3 | convolution fusion | flops 50593792 | bytes 3676160 | tf_op jit(solution)/shard_map/dot_general | solution.py:67
  39.0 1.1 %fusion.31 = bf16[32,8192]{1,0:T(8,128)(2,1)S(1)} fusion(f32[8192,32]{0,1:T(8,128)S(1)} %convolution_add_fusion.1, bf16[32,96]{1,0:T(8,128)(2,1)S(1)} %reshape.205, bf16[12,8,64,128]{3,2,1,0:T(8,128)(2,1)S(1)} %bitcast.234, f32[32]{0:T(128)S(1)} %copy-done.6), kind=kOutput, calls=%fused_computation.49 | convolution fusion | flops 51904512 | bytes 3152000 | tf_op jit(solution)/shard_map/dot_general | solution.py:67
  40.1 2.4 %copy.198 = f32[32,8192]{0,1:T(8,128)} copy(bf16[32,8192]{1,0:T(8,128)(2,1)S(1)} %fusion.31) | data formatting | bytes 1572864 | tf_op jit(solution)/shard_map/convert_element_type | solution.py:75
  42.5 4.8 %reduce_sum.18 = f32[32,4,4,64]{0,3,2,1:T(8,128)S(1)} reduce(f32[32,4,2,4,2,64,2]{0,6,5,4,3,2,1:T(2,128)} %bitcast.225, f32[]{:T(128)} %constant.36.clone.1), dimensions={2,4,6}, to_apply=%region_0.1 | reduce | flops 229376 | bytes 1179652 | tf_op jit(solution)/shard_map/reduce_sum | solution.py:78
  47.4 2.1 %collective-permute-start.5 = (bf16[32,1,4,64]{0,3,2,1:T(8,128)(2,1)S(1)}, bf16[32,1,4,64]{0,3,2,1:T(8,128)(2,1)S(1)}, u32[]{:S(2)}, u32[]{:S(2)}) collective-permute-start(bf16[32,1,4,64]{0,3,2,1:T(8,128)(2,1)S(1)} %get-tuple-element.101), channel_id=1, source_target_pairs={{8,0},{16,8},{24,16},{0,24},{9,1},{17,9},{25,17},{1,25},{10,2},{18... | collective-permute-start | bytes 49160 | tf_op jit(solution)/shard_map/ppermute | solution.py:27
  49.6 2.2 %collective-permute-done.5 = bf16[32,1,4,64]{0,3,2,1:T(8,128)(2,1)S(1)} collective-permute-done((bf16[32,1,4,64]{0,3,2,1:T(8,128)(2,1)S(1)}, bf16[32,1,4,64]{0,3,2,1:T(8,128)(2,1)S(1)}, u32[]{:S(2)}, u32[]{:S(2)}) %collective-permute-start.5) | collective-permute-done | bytes 16416 | tf_op jit(solution)/shard_map/ppermute | solution.py:27
  51.8 2.9 %collective-permute-done.4 = bf16[32,1,4,64]{0,3,2,1:T(8,128)(2,1)S(1)} collective-permute-done((bf16[32,1,4,64]{0,3,2,1:T(8,128)(2,1)S(1)}, bf16[32,1,4,64]{0,3,2,1:T(8,128)(2,1)S(1)}, u32[]{:S(2)}, u32[]{:S(2)}) %collective-permute-start.4) | collective-permute-done | bytes 16416 | tf_op jit(solution)/shard_map/ppermute | solution.py:25
  55.3 2.5 %collective-permute-done.7 = bf16[32,6,1,64]{0,3,2,1:T(8,128)(2,1)S(1)} collective-permute-done((bf16[32,6,1,64]{0,3,2,1:T(8,128)(2,1)S(1)}, bf16[32,6,1,64]{0,3,2,1:T(8,128)(2,1)S(1)}, u32[]{:S(2)}, u32[]{:S(2)}) %collective-permute-start.7) | collective-permute-done | bytes 24608 | tf_op jit(solution)/shard_map/ppermute | solution.py:27
  57.8 2.9 %collective-permute-done.6 = bf16[32,6,1,64]{0,3,2,1:T(8,128)(2,1)S(1)} collective-permute-done((bf16[32,6,1,64]{0,3,2,1:T(8,128)(2,1)S(1)}, bf16[32,6,1,64]{0,3,2,1:T(8,128)(2,1)S(1)}, u32[]{:S(2)}, u32[]{:S(2)}) %collective-permute-start.6) | collective-permute-done | bytes 24608 | tf_op jit(solution)/shard_map/ppermute | solution.py:25
  67.9 8.0 %all_to_all.18 = bf16[8,2,512]{2,1,0:T(2,128)(2,1)S(1)} all-to-all(bf16[8,2,512]{2,1,0:T(2,128)(2,1)S(1)} %reshape.247), channel_id=1, replica_groups=mesh['gx'=4,'gy'=8] {'gy'}, dimensions={0} | all-to-all | bytes 32768 | tf_op jit(solution)/shard_map/all_to_all | solution.py:88
  76.2 4.7 %collective-permute-done.8 = bf16[64,2,16,4]{0,2,3,1:T(8,128)(2,1)S(1)} collective-permute-done((bf16[64,2,16,4]{0,2,3,1:T(8,128)(2,1)S(1)}, bf16[64,2,16,4]{0,2,3,1:T(8,128)(2,1)S(1)}, u32[]{:S(2)}, u32[]{:S(2)}) %collective-permute-start.8) | collective-permute-done | bytes 16416 | tf_op jit(solution)/shard_map/ppermute | solution.py:12
  80.9 4.8 %collective-permute-done.9 = bf16[64,2,16,4]{0,2,3,1:T(8,128)(2,1)S(1)} collective-permute-done((bf16[64,2,16,4]{0,2,3,1:T(8,128)(2,1)S(1)}, bf16[64,2,16,4]{0,2,3,1:T(8,128)(2,1)S(1)}, u32[]{:S(2)}, u32[]{:S(2)}) %collective-permute-start.9) | collective-permute-done | bytes 16416 | tf_op jit(solution)/shard_map/ppermute | solution.py:12
  87.6 2.9 %collective-permute-done.10 = bf16[64,2,16,4]{0,2,3,1:T(8,128)(2,1)S(1)} collective-permute-done((bf16[64,2,16,4]{0,2,3,1:T(8,128)(2,1)S(1)}, bf16[64,2,16,4]{0,2,3,1:T(8,128)(2,1)S(1)}, u32[]{:S(2)}, u32[]{:S(2)}) %collective-permute-start.10) | collective-permute-done | bytes 16416 | tf_op jit(solution)/shard_map/ppermute | solution.py:12
  91.2 1.1 %collective-permute-done.12 = bf16[64,8,16,1]{0,2,3,1:T(8,128)(2,1)S(1)} collective-permute-done((bf16[64,8,16,1]{0,2,3,1:T(8,128)(2,1)S(1)}, bf16[64,8,16,1]{0,2,3,1:T(8,128)(2,1)S(1)}, u32[]{:S(2)}, u32[]{:S(2)}) %collective-permute-start.12) | collective-permute-done | bytes 16416 | tf_op jit(solution)/shard_map/ppermute | solution.py:27
  92.3 3.9 %collective-permute-done.11 = bf16[64,8,16,1]{0,2,3,1:T(8,128)(2,1)S(1)} collective-permute-done((bf16[64,8,16,1]{0,2,3,1:T(8,128)(2,1)S(1)}, bf16[64,8,16,1]{0,2,3,1:T(8,128)(2,1)S(1)}, u32[]{:S(2)}, u32[]{:S(2)}) %collective-permute-start.11) | collective-permute-done | bytes 16416 | tf_op jit(solution)/shard_map/ppermute | solution.py:25
  (157 shorter events, 27.2 us)
Async XLA Ops:
  0.6 7.8 %copy-start = (bf16[32,8,8,128]{3,2,1,0:T(8,128)(2,1)S(1)}, bf16[32,8,8,128]{3,2,1,0:T(8,128)(2,1)}, u32[]{:S(2)}) copy-start(bf16[32,8,8,128]{3,2,1,0:T(8,128)(2,1)} %param.7) | copy-start | bytes 1572868
  0.6 11.5 %copy-start.2 = (bf16[27,32,32]{2,1,0:T(8,128)(2,1)S(1)}, bf16[27,32,32]{2,1,0:T(8,128)(2,1)}, u32[]{:S(2)}) copy-start(bf16[27,32,32]{2,1,0:T(8,128)(2,1)} %param.8) | copy-start | bytes 165892
  2.1 6.3 %collective-permute-start = (bf16[32,1,8,128]{3,0,2,1:T(8,128)(2,1)S(1)}, bf16[32,1,8,128]{3,0,2,1:T(8,128)(2,1)S(1)}, u32[]{:S(2)}, u32[]{:S(2)}) collective-permute-start(bf16[32,1,8,128]{3,0,2,1:T(8,128)(2,1)S(1)} %get-tuple-element.57), channel_id=1, source_target_pairs={{0,8},{8,16},{16,24},{24,0},{1,9},{9,17},{17,25},{25,1},{2,10},{10... | collective-permute-start | bytes 196616 | tf_op jit(solution)/shard_map/ppermute | solution.py:25
  5.1 4.7 %collective-permute-start.1 = (bf16[32,1,8,128]{3,0,2,1:T(8,128)(2,1)S(1)}, bf16[32,1,8,128]{3,0,2,1:T(8,128)(2,1)S(1)}, u32[]{:S(2)}, u32[]{:S(2)}) collective-permute-start(bf16[32,1,8,128]{3,0,2,1:T(8,128)(2,1)S(1)} %get-tuple-element.56), channel_id=1, source_target_pairs={{8,0},{16,8},{24,16},{0,24},{9,1},{17,9},{25,17},{1,25},{10,2},{18... | collective-permute-start | bytes 196616 | tf_op jit(solution)/shard_map/ppermute | solution.py:27
  9.9 4.3 %collective-permute-start.3 = (bf16[32,10,1,128]{3,0,2,1:T(8,128)(2,1)S(1)}, bf16[32,10,1,128]{3,0,2,1:T(8,128)(2,1)S(1)}, u32[]{:S(2)}, u32[]{:S(2)}) collective-permute-start(bf16[32,10,1,128]{3,0,2,1:T(8,128)(2,1)S(1)} %get-tuple-element.52), channel_id=1, source_target_pairs={{1,0},{2,1},{3,2},{4,3},{5,4},{6,5},{7,6},{0,7},{9,8},{10,9},{11,1... | collective-permute-start | bytes 245768 | tf_op jit(solution)/shard_map/ppermute | solution.py:27
  12.1 5.7 %collective-permute-start.2 = (bf16[32,10,1,128]{3,0,2,1:T(8,128)(2,1)S(1)}, bf16[32,10,1,128]{3,0,2,1:T(8,128)(2,1)S(1)}, u32[]{:S(2)}, u32[]{:S(2)}) collective-permute-start(bf16[32,10,1,128]{3,0,2,1:T(8,128)(2,1)S(1)} %get-tuple-element.51), channel_id=1, source_target_pairs={{0,1},{1,2},{2,3},{3,4},{4,5},{5,6},{6,7},{7,0},{8,9},{9,10},{10,1... | collective-permute-start | bytes 245768 | tf_op jit(solution)/shard_map/ppermute | solution.py:25
  37.8 1.1 %copy-start.6 = (f32[32]{0:T(128)S(1)}, f32[32]{0:T(128)}, u32[]{:S(2)}) copy-start(f32[32]{0:T(128)} %param.9) | copy-start | bytes 388
  47.4 7.9 %copy-start.3 = (bf16[27,64,32]{1,2,0:T(8,128)(2,1)S(1)}, bf16[27,64,32]{1,2,0:T(8,128)(2,1)}, u32[]{:S(2)}) copy-start(bf16[27,64,32]{1,2,0:T(8,128)(2,1)} %param.10) | copy-start | bytes 331780
  47.4 4.4 %collective-permute-start.5 = (bf16[32,1,4,64]{0,3,2,1:T(8,128)(2,1)S(1)}, bf16[32,1,4,64]{0,3,2,1:T(8,128)(2,1)S(1)}, u32[]{:S(2)}, u32[]{:S(2)}) collective-permute-start(bf16[32,1,4,64]{0,3,2,1:T(8,128)(2,1)S(1)} %get-tuple-element.101), channel_id=1, source_target_pairs={{8,0},{16,8},{24,16},{0,24},{9,1},{17,9},{25,17},{1,25},{10,2},{18... | collective-permute-start | bytes 49160 | tf_op jit(solution)/shard_map/ppermute | solution.py:27
  49.5 5.2 %collective-permute-start.4 = (bf16[32,1,4,64]{0,3,2,1:T(8,128)(2,1)S(1)}, bf16[32,1,4,64]{0,3,2,1:T(8,128)(2,1)S(1)}, u32[]{:S(2)}, u32[]{:S(2)}) collective-permute-start(bf16[32,1,4,64]{0,3,2,1:T(8,128)(2,1)S(1)} %get-tuple-element.100), channel_id=1, source_target_pairs={{0,8},{8,16},{16,24},{24,0},{1,9},{9,17},{17,25},{25,1},{2,10},{10... | collective-permute-start | bytes 49160 | tf_op jit(solution)/shard_map/ppermute | solution.py:25
  54.7 3.1 %collective-permute-start.7 = (bf16[32,6,1,64]{0,3,2,1:T(8,128)(2,1)S(1)}, bf16[32,6,1,64]{0,3,2,1:T(8,128)(2,1)S(1)}, u32[]{:S(2)}, u32[]{:S(2)}) collective-permute-start(bf16[32,6,1,64]{0,3,2,1:T(8,128)(2,1)S(1)} %get-tuple-element.76), channel_id=1, source_target_pairs={{1,0},{2,1},{3,2},{4,3},{5,4},{6,5},{7,6},{0,7},{9,8},{10,9},{11,1... | collective-permute-start | bytes 73736 | tf_op jit(solution)/shard_map/ppermute | solution.py:27
  54.8 5.9 %collective-permute-start.6 = (bf16[32,6,1,64]{0,3,2,1:T(8,128)(2,1)S(1)}, bf16[32,6,1,64]{0,3,2,1:T(8,128)(2,1)S(1)}, u32[]{:S(2)}, u32[]{:S(2)}) collective-permute-start(bf16[32,6,1,64]{0,3,2,1:T(8,128)(2,1)S(1)} %get-tuple-element.75), channel_id=1, source_target_pairs={{0,1},{1,2},{2,3},{3,4},{4,5},{5,6},{6,7},{7,0},{8,9},{9,10},{10,1... | collective-permute-start | bytes 73736 | tf_op jit(solution)/shard_map/ppermute | solution.py:25
  66.2 0.8 copy-start.4
  66.7 19.0 %copy-start.1 = (bf16[27,128,64]{1,2,0:T(8,128)(2,1)S(1)}, bf16[27,128,64]{1,2,0:T(8,128)(2,1)}, u32[]{:S(2)}) copy-start(bf16[27,128,64]{1,2,0:T(8,128)(2,1)} %param.12) | copy-start | bytes 1327108
  76.0 4.9 %collective-permute-start.8 = (bf16[64,2,16,4]{0,2,3,1:T(8,128)(2,1)S(1)}, bf16[64,2,16,4]{0,2,3,1:T(8,128)(2,1)S(1)}, u32[]{:S(2)}, u32[]{:S(2)}) collective-permute-start(bf16[64,2,16,4]{0,2,3,1:T(8,128)(2,1)S(1)} %bitcast.247), channel_id=1, source_target_pairs={{0,8},{8,16},{16,24},{24,0},{1,9},{9,17},{17,25},{25,1},{2,10},{10... | collective-permute-start | bytes 49160 | tf_op jit(solution)/shard_map/ppermute | solution.py:12
  80.9 4.8 %collective-permute-start.9 = (bf16[64,2,16,4]{0,2,3,1:T(8,128)(2,1)S(1)}, bf16[64,2,16,4]{0,2,3,1:T(8,128)(2,1)S(1)}, u32[]{:S(2)}, u32[]{:S(2)}) collective-permute-start(bf16[64,2,16,4]{0,2,3,1:T(8,128)(2,1)S(1)} %collective-permute-done.8), channel_id=1, source_target_pairs={{0,8},{8,16},{16,24},{24,0},{1,9},{9,17},{17,25},{25,1},{2,10},{10... | collective-permute-start | bytes 49160 | tf_op jit(solution)/shard_map/ppermute | solution.py:12
  85.7 4.8 %collective-permute-start.10 = (bf16[64,2,16,4]{0,2,3,1:T(8,128)(2,1)S(1)}, bf16[64,2,16,4]{0,2,3,1:T(8,128)(2,1)S(1)}, u32[]{:S(2)}, u32[]{:S(2)}) collective-permute-start(bf16[64,2,16,4]{0,2,3,1:T(8,128)(2,1)S(1)} %collective-permute-done.9), channel_id=1, source_target_pairs={{0,8},{8,16},{16,24},{24,0},{1,9},{9,17},{17,25},{25,1},{2,10},{10... | collective-permute-start | bytes 49160 | tf_op jit(solution)/shard_map/ppermute | solution.py:12
  90.7 1.7 %collective-permute-start.12 = (bf16[64,8,16,1]{0,2,3,1:T(8,128)(2,1)S(1)}, bf16[64,8,16,1]{0,2,3,1:T(8,128)(2,1)S(1)}, u32[]{:S(2)}, u32[]{:S(2)}) collective-permute-start(bf16[64,8,16,1]{0,2,3,1:T(8,128)(2,1)S(1)} %get-tuple-element.96), channel_id=1, source_target_pairs={{1,0},{2,1},{3,2},{4,3},{5,4},{6,5},{7,6},{0,7},{9,8},{10,9},{11,1... | collective-permute-start | bytes 49160 | tf_op jit(solution)/shard_map/ppermute | solution.py:27
  90.7 5.5 %collective-permute-start.11 = (bf16[64,8,16,1]{0,2,3,1:T(8,128)(2,1)S(1)}, bf16[64,8,16,1]{0,2,3,1:T(8,128)(2,1)S(1)}, u32[]{:S(2)}, u32[]{:S(2)}) collective-permute-start(bf16[64,8,16,1]{0,2,3,1:T(8,128)(2,1)S(1)} %get-tuple-element.95), channel_id=1, source_target_pairs={{0,1},{1,2},{2,3},{3,4},{4,5},{5,6},{6,7},{7,0},{8,9},{9,10},{10,1... | collective-permute-start | bytes 49160 | tf_op jit(solution)/shard_map/ppermute | solution.py:25
  102.3 0.9 copy-start.5
